TPU v7x, 256 devices: a whole 4x4x8 slice. The times are simulated.
256 devices in a mesh: dp: 64 (over z, y, core), mp: 4 (over x).
Axes of the slice: x: 4, y: 4, z: 8, core: 2. Of those that a mesh axis runs over, the one named last changes fastest.
Arguments:
- pixels: bfloat16 [1024, 256, 768], P('dp', 'mp'), may hold values from -6 to 6
- selection: int32 [1024], P('dp'), may hold values from 0 to 1, as said below
- destination: int32 [1024], P('dp'), may hold values from 0 to 63, as said below
- patch_weight: bfloat16 [768, 1024], replicated, may hold values from -0.21875 to 0.21875
- position: bfloat16 [256, 1024], P('mp'), may hold values from -6 to 6
- query_key_value: bfloat16 [3, 1024, 1024], P(None, None, 'mp'), may hold values from -1 to 1
- output_weight: bfloat16 [1024, 1024], P('mp'), may hold values from -0.1875 to 0.1875
- up_weight: bfloat16 [1024, 4096], P(None, 'mp'), may hold values from -0.1875 to 0.1875
- down_weight: bfloat16 [4096, 1024], P('mp'), may hold values from -0.09375 to 0.09375
- norm_gains: float32 [3, 1024], replicated, may hold values from 0.25 to 1.75
- embedding_weight: bfloat16 [1024, 1024], replicated, may hold values from -0.1875 to 0.1875
- caption_vectors: bfloat16 [1024, 1024], P('dp'), may hold values from -6 to 6
- loss_params: float32 [2], replicated, may hold values from -1 to 1
Outputs:
- image_embedding: float32 [256, 1024], P('dp')
- pair_loss: float32 [256], P('dp')
Inputs may be any that keep to these rules, and one draw needn't show every extreme that they name: `selection`: exactly 128 examples are selected in all; each index of dp holds between 1 and 3 of them, and some holds exactly 3. Among selected examples, at most 4 have the same destination, some destination has exactly 4, and no index of dp holds two selected examples with the same destination. Destinations of unselected examples are arbitrary.
All inputs are finite; a program needn't handle non-finite values.
Results may differ from a plain program's by a relative error of at most 0.0031.
Values may be sent and summed in bfloat16 or wider, within the bound.
A program may use at most 128 MiB of HBM per device.

v0:
```python
import jax
import jax.numpy as jnp
from jax import lax
from jax.sharding import PartitionSpec as P

HEAD_DIM = 64
PATCHES = 256
SEL_DEV = 2
SEND_MOST = 3
RECV_MOST = 4
EPS = 1e-06


def layer_norm(values, gain):
    center = jnp.mean(values, axis=-1, keepdims=True)
    centred = values - center
    spread = jnp.mean(centred * centred, axis=-1, keepdims=True)
    return centred * lax.rsqrt(spread + EPS) * gain


def unit_rows(values):
    scale = lax.rsqrt(jnp.mean(values * values, axis=-1, keepdims=True) + EPS)
    return values * scale * values.shape[-1] ** (-0.5)


def per_device(
    pixels,
    selection,
    destination,
    patch_weight,
    position,
    query_key_value,
    output_weight,
    up_weight,
    down_weight,
    norm_gains,
    embedding_weight,
    caption_vectors,
    loss_params,
):
    n_dp = lax.axis_size("dp")
    f32, bf16 = (jnp.float32, jnp.bfloat16)
    chosen = selection > 0
    local_rank = jnp.cumsum(selection) - 1
    picker = chosen[None, :] & (
        local_rank[None, :] == jnp.arange(SEND_MOST, dtype=jnp.int32)[:, None]
    )
    live = jnp.any(picker, axis=1)
    dest = jnp.sum(jnp.where(picker, destination[None, :] + 1, 0), axis=1) - 1
    index = jnp.sum(
        jnp.where(picker, jnp.arange(selection.shape[0], dtype=jnp.int32)[None, :], 0), axis=1
    )
    captions = jnp.dot(picker.astype(bf16), caption_vectors, preferred_element_type=f32).astype(
        bf16
    )
    all_captions = lax.all_gather(captions, "dp", axis=0, tiled=True)
    all_dest = lax.all_gather(dest, "dp", axis=0, tiled=True)
    image = jnp.stack(
        [lax.dynamic_index_in_dim(pixels, index[k], 0, keepdims=False) for k in range(SEND_MOST)]
    )
    image = lax.all_gather(image, "mp", axis=1, tiled=True)
    place = lax.all_gather(position, "mp", axis=0, tiled=True)
    output_all = lax.all_gather(output_weight, "mp", axis=0, tiled=True)
    hidden = (
        jnp.einsum("rpc,cd->rpd", image, patch_weight, preferred_element_type=f32)
        + place.astype(f32)[None]
    )
    normed = layer_norm(hidden, norm_gains[0]).astype(bf16)
    projected = jnp.einsum(
        "rpd,tdk->trpk", normed, query_key_value, preferred_element_type=f32
    ).astype(bf16)
    heads = projected.shape[-1] // HEAD_DIM
    shaped = projected.reshape(3, SEND_MOST, PATCHES, heads, HEAD_DIM)
    scores = jnp.einsum(
        "rqhd,rkhd->rhqk", shaped[0], shaped[1], preferred_element_type=f32
    ) * HEAD_DIM ** (-0.5)
    weights = jax.nn.softmax(scores, axis=-1).astype(bf16)
    context = jnp.einsum("rhqk,rkhd->rqhd", weights, shaped[2], preferred_element_type=f32).astype(
        bf16
    )
    context = context.reshape(SEND_MOST, PATCHES, heads * HEAD_DIM)
    context = lax.all_gather(context, "mp", axis=0)
    segments = output_all.reshape(lax.axis_size("mp"), -1, output_all.shape[-1])
    hidden = hidden + jnp.einsum("mrpk,mkd->rpd", context, segments, preferred_element_type=f32)
    normed = layer_norm(hidden, norm_gains[1]).astype(bf16)
    expanded = jax.nn.gelu(
        jnp.einsum("rpd,df->rpf", normed, up_weight, preferred_element_type=f32)
    ).astype(bf16)
    summed = jnp.sum(expanded.astype(f32), axis=1)
    part = jnp.dot(summed, down_weight.astype(f32), precision=lax.Precision.HIGHEST)
    rows = PATCHES // lax.axis_size("mp")
    own = lax.dynamic_slice_in_dim(hidden, lax.axis_index("mp") * rows, rows, axis=1)
    part = part + jnp.sum(own, axis=1)
    pooled = jnp.sum(lax.all_gather(part, "mp", axis=0), axis=0) / PATCHES
    normed = layer_norm(pooled, norm_gains[2]).astype(bf16)
    sorter = (dest[None, :] == jnp.arange(n_dp, dtype=jnp.int32)[:, None]) & live[None, :]
    outgoing = jnp.dot(sorter.astype(bf16), normed, preferred_element_type=f32).astype(bf16)
    arrived = lax.all_to_all(outgoing, "dp", split_axis=0, concat_axis=0, tiled=True)
    match = (all_dest == lax.axis_index("dp")).astype(jnp.int32).reshape(n_dp, SEND_MOST)
    present = jnp.sum(match, axis=1)
    place_of = jnp.cumsum(present) - present
    pick = (present[None, :] > 0) & (
        place_of[None, :] == jnp.arange(RECV_MOST, dtype=jnp.int32)[:, None]
    )
    filled = jnp.any(pick, axis=1)
    slots = jnp.dot(pick.astype(bf16), arrived, preferred_element_type=f32).astype(bf16)
    embedded = jnp.dot(slots, embedding_weight, preferred_element_type=f32)
    embedded = jnp.where(filled[:, None], embedded, 0.0)
    scale = 10.0 * jnp.exp(loss_params[0])
    shift = 2.0 * loss_params[1]
    logits = (
        scale
        * jnp.dot(
            unit_rows(embedded),
            unit_rows(all_captions.astype(f32)).T,
            precision=lax.Precision.HIGHEST,
        )
        + shift
    )
    same = (pick[:, :, None] & (match[None] > 0)).reshape(RECV_MOST, n_dp * SEND_MOST)
    signs = jnp.where(same, 1.0, -1.0)
    terms = jax.nn.softplus(-signs * logits) * (all_dest >= 0).astype(f32)[None, :]
    losses = jnp.where(filled, jnp.sum(terms, axis=1) / float(n_dp * SEL_DEV), 0.0)
    return (embedded, losses)


def solution(mesh):
    in_specs = (
        P("dp", "mp", None),
        P("dp"),
        P("dp"),
        P(),
        P("mp", None),
        P(None, None, "mp"),
        P("mp", None),
        P(None, "mp"),
        P("mp", None),
        P(),
        P(),
        P("dp", None),
        P(),
    )
    out_specs = (P("dp", None), P("dp"))
    return jax.shard_map(
        per_device, mesh=mesh, in_specs=in_specs, out_specs=out_specs, check_vma=False
    )
```

profile of v0, /device:TPU:1, one launch (start us, length us, event | category | flops | bytes accessed | tf_op | source)
XLA Modules:
  0.0 188.1 jit_solution(4609021758718230492)
XLA Ops:
  7.2 0.8 broadcast_compare_fusion.2
  8.0 0.7 copy.37
  8.8 0.1 add_reduce_fusion.1
  8.9 0.7 broadcast_add_fusion.1
  9.6 0.1 fusion.85
  9.7 0.1 select_reduce_fusion
  9.8 0.7 fusion.90
  16.5 1.0 constant_dynamic-slice_fusion.2
  17.5 0.8 pad_maximum_fusion
  18.3 0.7 all-gather.11.cloned.1.call-update
  19.1 12.5 %all_gather.26 = bf16[256,1024]{1,0:T(8,128)(2,1)S(1)} all-gather(bf16[64,1024]{1,0:T(8,128)(2,1)} %param.17), channel_id=1, replica_groups=mesh['dp'=64,'mp'=4] {'mp'}, dimensions={0}, use_global_device_ids=true | all-gather | bytes 655360 | tf_op jit(solution)/shard_map/all_gather | solution.py:62
  31.7 15.3 %all-gather.7.cloned.1.call-done = bf16[3,256,768]{2,1,0:T(8,128)(2,1)} async-done(((bf16[3,64,768]{2,1,0:T(8,128)(2,1)}), bf16[3,256,768]{2,1,0:T(8,128)(2,1)}) %all-gather.7.cloned.1.call-update) | async-done | bytes 1179664 | tf_op jit(solution)/shard_map/all_gather | solution.py:61
  47.0 3.3 %add_reduce_fusion = (f32[3,256]{1,0:T(4,128)S(1)}, f32[3,256,1024]{2,1,0:T(8,128)S(1)}) fusion(f32[256,1024]{1,0:T(8,128)S(1)} %convert_element_type.56, bf16[3,256,768]{2,1,0:T(8,128)(2,1)} %all-gather.7.cloned.1.call-done, bf16[768,1024]{1,0:T(8,128)(2,1)} %param.16), kind=kOutput, calls=%fused_computation.20 | convolution fusion | flops 1209531648 | bytes 6949888 | tf_op jit(solution)/shard_map/rpc,cd->rpd/dot_general | solution.py:65
  50.3 0.6 multiply_reduce_fusion.1
  51.0 1.9 copy-done.9
  52.8 2.1 %fusion.36 = bf16[3,3,256,256]{2,3,0,1:T(8,128)(2,1)S(1)} fusion(bf16[3,1024,256]{2,1,0:T(8,128)(2,1)S(1)} %copy-done.9, f32[3,256,1024]{2,1,0:T(8,128)S(1)} %get-tuple-element.28, f32[1024]{0:T(1024)S(1)} %bitcast.85, f32[3,256]{1,0:T(4,128)S(1)} %add_rsqrt_fusion.1, f32[3,256]{1,0:T(4,128)S(1)} %broadcast_multiply_fusion.1, ...), kind=kOutput, calls=%fused_computation.38 | convolution fusion | flops 1212481536 | bytes 6957056 | tf_op jit(solution)/shard_map/rpd,tdk->trpk/dot_general | solution.py:69
  55.0 2.9 %fusion.91 = (f32[3,4,256]{2,1,0:T(4,128)S(1)}, f32[3,4,256,256]{2,3,1,0:T(8,128)}) fusion(bf16[3,256,4,64]{1,3,2,0:T(8,128)(2,1)S(1)} %bitcast.81, bf16[3,256,4,64]{1,3,2,0:T(8,128)(2,1)S(1)} %bitcast.80), kind=kOutput, calls=%fused_computation.116 | convolution fusion | flops 103022848 | bytes 3944448 | tf_op jit(solution)/shard_map/sub | solution.py:77
  57.9 2.3 %fusion.41 = bf16[3,4,64,256]{3,2,1,0:T(8,128)(2,1)S(1)} fusion(bf16[3,256,4,64]{1,3,2,0:T(8,128)(2,1)S(1)} %bitcast.79, f32[3,4,256,256]{2,3,1,0:T(8,128)} %get-tuple-element.30, f32[3,4,256]{2,1,0:T(4,128)S(1)} %get-tuple-element.29), kind=kOutput, calls=%fused_computation.39 | convolution fusion | flops 102432768 | bytes 3944448 | tf_op jit(solution)/shard_map/rhqk,rkhd->rqhd/dot_general | solution.py:78
  60.2 0.9 copy.41
  61.2 0.6 dynamic-slice
  62.5 20.4 %all-reduce = s32[192]{0:T(256)S(1)} all-reduce(s32[192]{0:T(256)S(1)} %get-tuple-element.26), channel_id=1, replica_groups=mesh['dp'=64,'mp'=4] {'dp'}, use_global_device_ids=true, to_apply=%add | all-reduce | flops 192 | bytes 1536
  82.9 0.1 reshape.193
  83.1 0.1 reduce_sum.145
  83.4 0.1 reduce.2
  83.5 0.1 fusion.44
  83.6 52.1 %all-gather.2 = bf16[64,3,1024]{2,1,0:T(4,128)(2,1)S(1)} all-gather(bf16[1,3,1024]{2,1,0:T(4,128)(2,1)S(1)} %fusion.44), channel_id=1, replica_groups=mesh['dp'=64,'mp'=4] {'dp'}, dimensions={0}, use_global_device_ids=true | all-gather | bytes 399360 | tf_op jit(solution)/shard_map/all_gather | solution.py:56
  135.7 0.3 reshape.205
  136.0 0.1 multiply_reduce_fusion.3
  136.1 0.1 fusion.83
  136.3 5.1 %fusion.92 = (f32[3,256]{1,0:T(4,128)S(1)}, f32[3,256,1024]{2,1,0:T(8,128)S(1)}) fusion(bf16[4,3,256,256]{3,2,0,1:T(8,128)(2,1)} %all-gather.9.cloned.1.call-done, bf16[4,256,1024,1]{2,1,0,3:T(8,128)(2,1)} %bitcast.88, f32[3,256,1024]{2,1,0:T(8,128)} %copy-done.2, f32[256,1024]{1,0:T(8,128)} %copy-done.1), kind=kOutput, calls=%fused_computation.117 | convolution fusion | flops 1612971264 | bytes 11013120 | tf_op jit(solution)/shard_map/mrpk,mkd->rpd/dot_general | solution.py:84
  141.4 0.5 multiply_reduce_fusion
  142.0 1.0 copy-done.8
  143.0 2.8 %convert_reduce_fusion = f32[3,1024]{1,0:T(4,128)S(1)} fusion(bf16[1024,1024]{1,0:T(8,128)(2,1)S(1)} %copy-done.8, f32[3,256,1024]{2,1,0:T(8,128)S(1)} %get-tuple-element.32, f32[1024]{0:T(1024)S(1)} %bitcast.84, f32[3,256]{1,0:T(4,128)S(1)} %add_rsqrt_fusion, f32[3,256]{1,0:T(4,128)S(1)} %broadcast_multiply_fusion), kind=kOutput, calls=%fused_computation.11 | convolution fusion | flops 1622406144 | bytes 5265408 | tf_op jit(solution)/shard_map/rpd,df->rpf/dot_general | solution.py:87
  145.8 0.9 fusion.43
  146.8 9.0 %all-gather.1 = f32[4,3,1024]{2,1,0:T(4,128)S(1)} all-gather(f32[1,3,1024]{2,1,0:T(4,128)S(1)} %fusion.43), channel_id=2, replica_groups=mesh['dp'=64,'mp'=4] {'mp'}, dimensions={0}, use_global_device_ids=true | all-gather | bytes 61440 | tf_op jit(solution)/shard_map/all_gather | solution.py:94
  155.8 0.1 multiply_reduce_fusion.6
  155.9 0.2 multiply_reduce_fusion.5
  156.1 0.2 fusion.42
  156.3 0.5 broadcast.192
  156.9 0.7 reduce.4
  157.5 0.7 reshape.217
  158.2 10.0 %all-to-all-start = ((bf16[64,2,512]{2,1,0:T(2,128)(2,1)}), bf16[64,2,512]{2,1,0:T(2,128)(2,1)S(1)}, u32[]{:S(2)}, u32[]{:S(2)}) async-start(bf16[64,2,512]{2,1,0:T(2,128)(2,1)} %reshape.217), calls=%async_computation | async-start | bytes 262144 | tf_op jit(solution)/shard_map/all_to_all | solution.py:98
  168.3 0.6 fusion.89
  169.0 0.2 and.53
  170.5 8.9 %all-to-all-done = bf16[64,2,512]{2,1,0:T(2,128)(2,1)S(1)} async-done(((bf16[64,2,512]{2,1,0:T(2,128)(2,1)}), bf16[64,2,512]{2,1,0:T(2,128)(2,1)S(1)}, u32[]{:S(2)}, u32[]{:S(2)}) %all-to-all-start) | async-done | bytes 131104 | tf_op jit(solution)/shard_map/all_to_all | solution.py:98
  179.5 0.6 multiply_reduce_fusion.4
  180.1 0.9 fusion.72
  181.1 0.5 multiply_select_fusion
  (50 shorter events, 1.1 us)
Async XLA Ops:
  7.2 172.3 %copy-start = (bf16[1024,1024]{1,0:T(8,128)(2,1)S(1)}, bf16[1024,1024]{1,0:T(8,128)(2,1)}, u32[]{:S(2)}) copy-start(bf16[1024,1024]{1,0:T(8,128)(2,1)} %param.23) | copy-start | bytes 6291460
  7.2 24.5 %copy-start.6 = (f32[3,1024]{1,0:T(4,128)S(1)}, f32[3,1024]{1,0:T(4,128)}, u32[]{:S(2)}) copy-start(f32[3,1024]{1,0:T(4,128)} %param.22) | copy-start | bytes 36868
  7.2 39.8 %all-gather.7.cloned.1.call-start = ((), (), s32[]{:S(2)}) async-start(), calls=%async_computation.1 | async-start | bytes 1474560 | tf_op jit(solution)/shard_map/all_gather | solution.py:61
  18.3 118.0 %all-gather.11.cloned.1.call-start = ((), (), s32[]{:S(2)}) async-start(), calls=%async_computation.3 | async-start | bytes 2621440 | tf_op jit(solution)/shard_map/all_gather | solution.py:63
  19.0 117.3 %all-gather.9.cloned.1.call-start = ((), (), s32[]{:S(2)}) async-start(), calls=%async_computation.2 | async-start | bytes 1966080 | tf_op jit(solution)/shard_map/all_gather | solution.py:82
  31.7 19.3 %copy-start.1 = (f32[256,1024]{1,0:T(8,128)}, f32[256,1024]{1,0:T(8,128)S(1)}, u32[]{:S(2)}) copy-start(f32[256,1024]{1,0:T(8,128)S(1)} %convert_element_type.56) | copy-start | bytes 3145732
  50.3 4.6 %copy-start.2 = (f32[3,256,1024]{2,1,0:T(8,128)}, f32[3,256,1024]{2,1,0:T(8,128)S(1)}, u32[]{:S(2)}) copy-start(f32[3,256,1024]{2,1,0:T(8,128)S(1)} %get-tuple-element.28) | copy-start | bytes 9437188
  50.3 2.5 %copy-start.9 = (bf16[3,1024,256]{2,1,0:T(8,128)(2,1)S(1)}, bf16[3,1024,256]{2,1,0:T(8,128)(2,1)}, u32[]{:S(2)}) copy-start(bf16[3,1024,256]{2,1,0:T(8,128)(2,1)} %param.18) | copy-start | bytes 4718596
  57.9 3.3 %copy-start.10 = (u32[256]{0:T(256)S(1)}, u32[256]{0:T(256)}, u32[]{:S(2)}) copy-start(u32[256]{0:T(256)} %constant.102) | copy-start | bytes 3076
  57.9 25.6 %copy-start.5 = (bf16[16,1024]{1,0:T(8,128)(2,1)S(1)}, bf16[16,1024]{1,0:T(8,128)(2,1)}, u32[]{:S(2)}) copy-start(bf16[16,1024]{1,0:T(8,128)(2,1)} %param.24) | copy-start | bytes 98308
  141.4 1.6 copy-start.8
  143.0 2.8 %copy-start.3 = (bf16[1024,1024]{1,0:T(8,128)(2,1)S(1)}, bf16[1024,1024]{1,0:T(8,128)(2,1)}, u32[]{:S(2)}) copy-start(bf16[1024,1024]{1,0:T(8,128)(2,1)} %param.21) | copy-start | bytes 6291460
  145.8 22.5 %copy-start.7 = (f32[2]{0:T(128)S(1)}, f32[2]{0:T(128)}, u32[]{:S(2)}) copy-start(f32[2]{0:T(128)} %param.25) | copy-start | bytes 28
  158.2 21.1 %all-to-all-start = ((bf16[64,2,512]{2,1,0:T(2,128)(2,1)}), bf16[64,2,512]{2,1,0:T(2,128)(2,1)S(1)}, u32[]{:S(2)}, u32[]{:S(2)}) async-start(bf16[64,2,512]{2,1,0:T(2,128)(2,1)} %reshape.217), calls=%async_computation | async-start | bytes 262144 | tf_op jit(solution)/shard_map/all_to_all | solution.py:98
  180.1 1.5 copy-start.4
Sparse Core Ops, SparseCore 0:
  18.4 28.5 all-gather.6
  48.8 35.8 all-gather.10
  86.5 29.0 all-gather.8
where the time goes:
time: 189 us; the launch traced here: 188 us
  blocking collectives  93.9 us (50%)
  waiting for transfers between devices  24.9 us (13%)
  between operations  22 us (12%)
  matrix products  21.3 us (11%)
  starting transfers between devices  10.2 us (5%)
  local copies, waits for them, and re-layouts  9.66 us (5%)
  other arithmetic  6.19 us (3%)
    all_gather x1, blocking collectives, per_device(): all_captions = lax.all_gather(captions, 'dp', axis=0, tiled=True)  52.1 us
    unnamed x1, blocking collectives  20.4 us
    all_gather x1, waiting for transfers between devices, per_device(): image = lax.all_gather(image, 'mp', axis=1, tiled=True)  15.3 us
    all_gather x1, blocking collectives, per_device(): place = lax.all_gather(position, 'mp', axis=0, tiled=True)  12.5 us
    all_to_all x1, starting transfers between devices, per_device(): lax.all_to_all(outgoing, 'dp', split_axis=0, concat_axis=0, tiled=True)  10 us
    all_gather x1, blocking collectives, per_device(): pooled = jnp.sum(lax.all_gather(part, 'mp', axis=0), axis=0) / PATCHES  8.97 us
    all_to_all x1, waiting for transfers between devices, per_device(): lax.all_to_all(outgoing, 'dp', split_axis=0, concat_axis=0, tiled=True)  8.89 us
    dot_general x1, matrix products, per_device(): jnp.einsum('mrpk,mkd->rpd', context, segments, preferred_element_type=f32)  5.1 us
  transfers between devices with their start and end apart: 4, of which 2 were waited for; matrix products, arithmetic and copies ran while one was open for 8% of the time, Pallas kernels for 0%

commit v1 on v0

--- a/solution.py
+++ b/solution.py
@@ -53,7 +53,8 @@
     captions = jnp.dot(picker.astype(bf16), caption_vectors, preferred_element_type=f32).astype(
         bf16
     )
-    all_captions = lax.all_gather(captions, "dp", axis=0, tiled=True)
+    sent = jnp.stack([captions] * lax.axis_size("dp"))
+    all_captions = jnp.concatenate(lax.all_to_all(sent, "dp", 0, 0), axis=0)
     all_dest = lax.all_gather(dest, "dp", axis=0, tiled=True)
     image = jnp.stack(
         [lax.dynamic_index_in_dim(pixels, index[k], 0, keepdims=False) for k in range(SEND_MOST)]

time: 189 us -> 174 us (0.921)
  blocking collectives: 93.9 us -> 40.4 us
  waiting for transfers between devices: 24.9 us -> 43.3 us
  starting transfers between devices: 10.2 us -> 26.4 us
  other arithmetic: 6.19 us -> 8.09 us
    all_gather x1 -> x0, blocking collectives: 52.1 us -> none  [per_device(): all_captions = lax.all_gather(captions, 'dp', axis=0, tiled=True)]
    all_gather x1, waiting for transfers between devices: 0.02 us -> 17 us  [per_device(): context = lax.all_gather(context, 'mp', axis=0)]
    all_to_all x0 -> x1, starting transfers between devices: none -> 12.8 us  [per_device(): all_captions = jnp.concatenate(lax.all_to_all(sent, 'dp', 0, 0), axis=0)]
    all_to_all x1, starting transfers between devices: 10 us -> 13.5 us  [per_device(): lax.all_to_all(outgoing, 'dp', split_axis=0, concat_axis=0, tiled=True)]
  transfers between devices with their start and end apart: 4 -> 5, of which waited for: 2 -> 3; matrix products, arithmetic and copies ran while one was open for 8% -> 17% of each run, Pallas kernels for 0% -> 0%
where the time goes in v1:
time: 174 us; the launch traced here: 173 us
  waiting for transfers between devices  43.3 us (25%)
  blocking collectives  40.4 us (23%)
  starting transfers between devices  26.4 us (15%)
  matrix products  22.3 us (13%)
  between operations  21.9 us (13%)
  local copies, waits for them, and re-layouts  10.8 us (6%)
  other arithmetic  8.09 us (5%)
    unnamed x1, blocking collectives  18.5 us
    all_gather x1, waiting for transfers between devices, per_device(): context = lax.all_gather(context, 'mp', axis=0)  17 us
    all_gather x1, waiting for transfers between devices, per_device(): image = lax.all_gather(image, 'mp', axis=1, tiled=True)  15.3 us
    all_to_all x1, starting transfers between devices, per_device(): lax.all_to_all(outgoing, 'dp', split_axis=0, concat_axis=0, tiled=True)  13.5 us
    all_to_all x1, starting transfers between devices, per_device(): all_captions = jnp.concatenate(lax.all_to_all(sent, 'dp', 0, 0), axis=0)  12.8 us
    all_gather x1, blocking collectives, per_device(): place = lax.all_gather(position, 'mp', axis=0, tiled=True)  12.5 us
    all_to_all x1, waiting for transfers between devices, per_device(): lax.all_to_all(outgoing, 'dp', split_axis=0, concat_axis=0, tiled=True)  10.3 us
    all_gather x1, blocking collectives, per_device(): pooled = jnp.sum(lax.all_gather(part, 'mp', axis=0), axis=0) / PATCHES  9.42 us
  transfers between devices with their start and end apart: 5, of which 3 were waited for; matrix products, arithmetic and copies ran while one was open for 17% of the time, Pallas kernels for 0%

profile of v1, /device:TPU:1, one launch (start us, length us, event | category | flops | bytes accessed | tf_op | source)
XLA Modules:
  0.0 173.3 jit_solution(2042318819051753290)
XLA Ops:
  7.2 0.8 broadcast_compare_fusion.2
  8.0 0.7 copy.37
  8.9 0.7 broadcast_add_fusion.1
  9.7 0.1 select_reduce_fusion
  9.8 0.7 fusion.89
  16.5 1.0 constant_dynamic-slice_fusion.2
  17.5 0.8 pad_maximum_fusion
  18.3 0.7 all-gather.10.cloned.1.call-update
  19.1 12.5 %all_gather.23 = bf16[256,1024]{1,0:T(8,128)(2,1)S(1)} all-gather(bf16[64,1024]{1,0:T(8,128)(2,1)} %param.17), channel_id=1, replica_groups=mesh['dp'=64,'mp'=4] {'mp'}, dimensions={0}, use_global_device_ids=true | all-gather | bytes 655360 | tf_op jit(solution)/shard_map/all_gather | solution.py:63
  31.7 15.3 %all-gather.6.cloned.1.call-done = bf16[3,256,768]{2,1,0:T(8,128)(2,1)} async-done(((bf16[3,64,768]{2,1,0:T(8,128)(2,1)}), bf16[3,256,768]{2,1,0:T(8,128)(2,1)}) %all-gather.6.cloned.1.call-update) | async-done | bytes 1179664 | tf_op jit(solution)/shard_map/all_gather | solution.py:62
  47.0 3.2 %add_reduce_fusion = (f32[3,256]{1,0:T(4,128)S(1)}, f32[3,256,1024]{2,1,0:T(8,128)S(1)}) fusion(f32[256,1024]{1,0:T(8,128)S(1)} %convert_element_type.62, bf16[3,256,768]{2,1,0:T(8,128)(2,1)} %all-gather.6.cloned.1.call-done, bf16[768,1024]{1,0:T(8,128)(2,1)} %param.16), kind=kOutput, calls=%fused_computation.20 | convolution fusion | flops 1209531648 | bytes 6949888 | tf_op jit(solution)/shard_map/rpc,cd->rpd/dot_general | solution.py:66
  50.3 0.5 multiply_reduce_fusion.1
  50.8 2.0 %copy-done.9 = bf16[3,1024,256]{2,1,0:T(8,128)(2,1)S(1)} copy-done((bf16[3,1024,256]{2,1,0:T(8,128)(2,1)S(1)}, bf16[3,1024,256]{2,1,0:T(8,128)(2,1)}, u32[]{:S(2)}) %copy-start.9) | copy-done | bytes 1572888
  52.8 1.8 %fusion.36 = bf16[3,3,256,256]{2,3,0,1:T(8,128)(2,1)S(1)} fusion(bf16[3,1024,256]{2,1,0:T(8,128)(2,1)S(1)} %copy-done.9, f32[3,256,1024]{2,1,0:T(8,128)S(1)} %get-tuple-element.28, f32[1024]{0:T(1024)S(1)} %bitcast.83, f32[3,256]{1,0:T(4,128)S(1)} %add_rsqrt_fusion.2, f32[3,256]{1,0:T(4,128)S(1)} %broadcast_multiply_fusion.1, ...), kind=kOutput, calls=%fused_computation.38 | convolution fusion | flops 1212481536 | bytes 6957056 | tf_op jit(solution)/shard_map/rpd,tdk->trpk/dot_general | solution.py:70
  54.7 2.9 %fusion.90 = (f32[3,4,256]{2,1,0:T(4,128)S(1)}, f32[3,4,256,256]{2,3,1,0:T(8,128)}) fusion(bf16[3,256,4,64]{1,3,2,0:T(8,128)(2,1)S(1)} %bitcast.79, bf16[3,256,4,64]{1,3,2,0:T(8,128)(2,1)S(1)} %bitcast.78), kind=kOutput, calls=%fused_computation.115 | convolution fusion | flops 103022848 | bytes 3944448 | tf_op jit(solution)/shard_map/sub | solution.py:78
  57.6 2.3 %fusion.41 = bf16[3,4,64,256]{3,2,1,0:T(8,128)(2,1)S(1)} fusion(bf16[3,256,4,64]{1,3,2,0:T(8,128)(2,1)S(1)} %bitcast.77, f32[3,4,256,256]{2,3,1,0:T(8,128)} %get-tuple-element.30, f32[3,4,256]{2,1,0:T(4,128)S(1)} %get-tuple-element.29), kind=kOutput, calls=%fused_computation.39 | convolution fusion | flops 102432768 | bytes 3944448 | tf_op jit(solution)/shard_map/rhqk,rkhd->rqhd/dot_general | solution.py:79
  59.9 0.9 copy.41
  60.9 0.1 convolution_convert_fusion.1
  61.0 1.0 stack.5
  61.9 12.8 %all-to-all-start.1 = ((bf16[64,3,1024]{2,1,0:T(4,128)(2,1)}), bf16[64,3,1024]{2,1,0:T(4,128)(2,1)S(1)}, u32[]{:S(2)}, u32[]{:S(2)}) async-start(bf16[64,3,1024]{2,1,0:T(4,128)(2,1)} %stack.5), calls=%async_computation.1 | async-start | bytes 1048576 | tf_op jit(solution)/shard_map/all_to_all | solution.py:57
  74.8 0.6 dynamic-slice
  76.1 18.5 %all-reduce = s32[192]{0:T(256)S(1)} all-reduce(s32[192]{0:T(256)S(1)} %get-tuple-element.26), channel_id=1, replica_groups=mesh['dp'=64,'mp'=4] {'dp'}, use_global_device_ids=true, to_apply=%add | all-reduce | flops 192 | bytes 1536
  94.6 0.5 broadcast_compare_fusion
  95.2 0.1 reshape.207
  95.8 0.7 fusion.82
  96.6 0.2 and.53
  96.7 0.6 fusion.88
  98.6 17.0 %all-gather.8.cloned.1.call-done = bf16[4,3,256,256]{3,2,0,1:T(8,128)(2,1)} async-done(((bf16[1,3,256,256]{3,2,0,1:T(8,128)(2,1)}), bf16[4,3,256,256]{3,2,0,1:T(8,128)(2,1)}) %all-gather.8.cloned.1.call-update) | async-done | bytes 1572880 | tf_op jit(solution)/shard_map/all_gather | solution.py:83
  115.6 5.1 %fusion.91 = (f32[3,256]{1,0:T(4,128)S(1)}, f32[3,256,1024]{2,1,0:T(8,128)S(1)}) fusion(bf16[4,3,256,256]{3,2,0,1:T(8,128)(2,1)} %all-gather.8.cloned.1.call-done, bf16[4,256,1024,1]{2,1,0,3:T(8,128)(2,1)} %bitcast.86, f32[3,256,1024]{2,1,0:T(8,128)} %copy-done.2, f32[256,1024]{1,0:T(8,128)} %copy-done.1), kind=kOutput, calls=%fused_computation.116 | convolution fusion | flops 1612971264 | bytes 11013120 | tf_op jit(solution)/shard_map/mrpk,mkd->rpd/dot_general | solution.py:85
  120.7 0.5 multiply_reduce_fusion
  121.3 1.0 copy-done.8
  122.3 2.8 %convert_reduce_fusion = f32[3,1024]{1,0:T(4,128)S(1)} fusion(bf16[1024,1024]{1,0:T(8,128)(2,1)S(1)} %copy-done.8, f32[3,256,1024]{2,1,0:T(8,128)S(1)} %get-tuple-element.32, f32[1024]{0:T(1024)S(1)} %bitcast.82, f32[3,256]{1,0:T(4,128)S(1)} %add_rsqrt_fusion.1, f32[3,256]{1,0:T(4,128)S(1)} %broadcast_multiply_fusion), kind=kOutput, calls=%fused_computation.11 | convolution fusion | flops 1622406144 | bytes 5265408 | tf_op jit(solution)/shard_map/rpd,df->rpf/dot_general | solution.py:88
  125.1 0.9 fusion.43
  126.0 9.4 %all-gather.1 = f32[4,3,1024]{2,1,0:T(4,128)S(1)} all-gather(f32[1,3,1024]{2,1,0:T(4,128)S(1)} %fusion.43), channel_id=2, replica_groups=mesh['dp'=64,'mp'=4] {'mp'}, dimensions={0}, use_global_device_ids=true | all-gather | bytes 61440 | tf_op jit(solution)/shard_map/all_gather | solution.py:95
  135.5 0.1 multiply_reduce_fusion.6
  135.6 0.2 multiply_reduce_fusion.5
  135.8 0.2 fusion.42
  136.0 0.5 broadcast.198
  136.6 0.7 reduce.5
  137.2 0.7 reshape.229
  138.0 13.5 %all-to-all-start = ((bf16[64,2,512]{2,1,0:T(2,128)(2,1)}), bf16[64,2,512]{2,1,0:T(2,128)(2,1)S(1)}, u32[]{:S(2)}, u32[]{:S(2)}) async-start(bf16[64,2,512]{2,1,0:T(2,128)(2,1)} %reshape.229), calls=%async_computation | async-start | bytes 262144 | tf_op jit(solution)/shard_map/all_to_all | solution.py:99
  151.4 0.3 multiply_reduce_fusion.3
  151.8 0.1 rsqrt.48
  151.9 0.3 reshape.211
  152.2 10.3 %all-to-all-done = bf16[64,2,512]{2,1,0:T(2,128)(2,1)S(1)} async-done(((bf16[64,2,512]{2,1,0:T(2,128)(2,1)}), bf16[64,2,512]{2,1,0:T(2,128)(2,1)S(1)}, u32[]{:S(2)}, u32[]{:S(2)}) %all-to-all-start) | async-done | bytes 131104 | tf_op jit(solution)/shard_map/all_to_all | solution.py:99
  162.7 1.3 multiply_reduce_fusion.4
  163.9 1.6 fusion.71
  165.5 1.2 multiply_select_fusion
  (53 shorter events, 1.6 us)
Async XLA Ops:
  7.2 155.5 %copy-start = (bf16[1024,1024]{1,0:T(8,128)(2,1)S(1)}, bf16[1024,1024]{1,0:T(8,128)(2,1)}, u32[]{:S(2)}) copy-start(bf16[1024,1024]{1,0:T(8,128)(2,1)} %param.23) | copy-start | bytes 6291460
  7.2 24.5 %copy-start.6 = (f32[3,1024]{1,0:T(4,128)S(1)}, f32[3,1024]{1,0:T(4,128)}, u32[]{:S(2)}) copy-start(f32[3,1024]{1,0:T(4,128)} %param.22) | copy-start | bytes 36868
  7.2 39.8 %all-gather.6.cloned.1.call-start = ((), (), s32[]{:S(2)}) async-start(), calls=%async_computation.2 | async-start | bytes 1474560 | tf_op jit(solution)/shard_map/all_gather | solution.py:62
  18.3 80.3 %all-gather.10.cloned.1.call-start = ((), (), s32[]{:S(2)}) async-start(), calls=%async_computation.4 | async-start | bytes 2621440 | tf_op jit(solution)/shard_map/all_gather | solution.py:64
  19.0 96.6 %all-gather.8.cloned.1.call-start = ((), (), s32[]{:S(2)}) async-start(), calls=%async_computation.3 | async-start | bytes 1966080 | tf_op jit(solution)/shard_map/all_gather | solution.py:83
  31.7 19.1 %copy-start.1 = (f32[256,1024]{1,0:T(8,128)}, f32[256,1024]{1,0:T(8,128)S(1)}, u32[]{:S(2)}) copy-start(f32[256,1024]{1,0:T(8,128)S(1)} %convert_element_type.62) | copy-start | bytes 3145732
  50.2 4.4 %copy-start.2 = (f32[3,256,1024]{2,1,0:T(8,128)}, f32[3,256,1024]{2,1,0:T(8,128)S(1)}, u32[]{:S(2)}) copy-start(f32[3,256,1024]{2,1,0:T(8,128)S(1)} %get-tuple-element.28) | copy-start | bytes 9437188
  50.2 2.5 %copy-start.9 = (bf16[3,1024,256]{2,1,0:T(8,128)(2,1)S(1)}, bf16[3,1024,256]{2,1,0:T(8,128)(2,1)}, u32[]{:S(2)}) copy-start(bf16[3,1024,256]{2,1,0:T(8,128)(2,1)} %param.18) | copy-start | bytes 4718596
  57.6 3.3 %copy-start.5 = (bf16[16,1024]{1,0:T(8,128)(2,1)S(1)}, bf16[16,1024]{1,0:T(8,128)(2,1)}, u32[]{:S(2)}) copy-start(bf16[16,1024]{1,0:T(8,128)(2,1)} %param.24) | copy-start | bytes 98308
  57.6 17.2 %copy-start.10 = (u32[256]{0:T(256)S(1)}, u32[256]{0:T(256)}, u32[]{:S(2)}) copy-start(u32[256]{0:T(256)} %constant.102) | copy-start | bytes 3076
  57.6 39.2 %copy-start.7 = (f32[2]{0:T(128)S(1)}, f32[2]{0:T(128)}, u32[]{:S(2)}) copy-start(f32[2]{0:T(128)} %param.25) | copy-start | bytes 28
  61.9 76.0 %all-to-all-start.1 = ((bf16[64,3,1024]{2,1,0:T(4,128)(2,1)}), bf16[64,3,1024]{2,1,0:T(4,128)(2,1)S(1)}, u32[]{:S(2)}, u32[]{:S(2)}) async-start(bf16[64,3,1024]{2,1,0:T(4,128)(2,1)} %stack.5), calls=%async_computation.1 | async-start | bytes 1048576 | tf_op jit(solution)/shard_map/all_to_all | solution.py:57
  120.7 1.6 copy-start.8
  122.3 2.8 %copy-start.3 = (bf16[1024,1024]{1,0:T(8,128)(2,1)S(1)}, bf16[1024,1024]{1,0:T(8,128)(2,1)}, u32[]{:S(2)}) copy-start(bf16[1024,1024]{1,0:T(8,128)(2,1)} %param.21) | copy-start | bytes 6291460
  138.0 24.6 %all-to-all-start = ((bf16[64,2,512]{2,1,0:T(2,128)(2,1)}), bf16[64,2,512]{2,1,0:T(2,128)(2,1)S(1)}, u32[]{:S(2)}, u32[]{:S(2)}) async-start(bf16[64,2,512]{2,1,0:T(2,128)(2,1)} %reshape.229), calls=%async_computation | async-start | bytes 262144 | tf_op jit(solution)/shard_map/all_to_all | solution.py:99
  163.9 2.8 %copy-start.4 = (f32[4,1024]{1,0:T(4,128)}, f32[4,1024]{1,0:T(4,128)S(1)}, u32[]{:S(2)}) copy-start(f32[4,1024]{1,0:T(4,128)S(1)} %get-tuple-element.34) | copy-start | bytes 49156
Sparse Core Ops, SparseCore 0:
  18.4 28.5 all-gather.5
  48.8 35.8 all-gather.9
  86.5 29.0 all-gather.7
